TPU v7x, 32 devices: a whole 2x2x4 slice. The times are simulated.
32 devices in a mesh: owner: 4 (over y, x), rows: 8 (over z, core).
Axes of the slice: x: 2, y: 2, z: 4, core: 2. Of those that a mesh axis runs over, the one named last changes fastest.
Arguments:
- train_gate: float32 [64, 2048, 1024], P('owner', 'rows'), may hold values from -0.1875 to 0.1875
- train_up: float32 [64, 2048, 1024], P('owner', 'rows'), may hold values from -0.1875 to 0.1875
- train_down: float32 [64, 1024, 2048], P('owner', None, 'rows'), may hold values from -0.25 to 0.25
- router_weight: float32 [2048, 64], P('rows', 'owner'), may hold values from -0.125 to 0.125
- router_gain: float32 [2048], P('rows'), may hold values from 0.25 to 1.75
Outputs:
- ready_gate: bfloat16 [64, 2048, 1024], P('owner', None, 'rows')
- ready_up: bfloat16 [64, 2048, 1024], P('owner', None, 'rows')
- ready_down: bfloat16 [64, 1024, 2048], P('owner', 'rows')
- scale_gate: float32 [64, 1024], P('owner', 'rows')
- scale_up: float32 [64, 1024], P('owner', 'rows')
- scale_down: float32 [64, 1024], P('owner', 'rows')
- serve_router: bfloat16 [2048, 64], replicated
All inputs are finite; a program needn't handle non-finite values. Where the computation divides by a largest or mean magnitude, that divisor is 1e-20 or more.
Results may differ from a plain program's by a relative error of at most 0.0013.
Values may be sent and summed in bfloat16 or wider, within the bound.
A program may use at most 192 MiB of HBM per device.

v0:
```python
import jax
import jax.numpy as jnp
from jax import lax
from jax.sharding import PartitionSpec as P

D_MODEL = 2048


def local(train_gate, train_up, train_down, router_weight, router_gain):
    total_gate, total_up, total_down = lax.psum(
        (
            jnp.sum(jnp.abs(train_gate), axis=1),
            jnp.sum(jnp.abs(train_up), axis=1),
            jnp.sum(jnp.abs(train_down), axis=2),
        ),
        "rows",
    )
    scale_gate = total_gate / D_MODEL
    scale_up = total_up / D_MODEL
    scale_down = total_down / D_MODEL
    narrow_gate, narrow_up, narrow_down = (
        (train_gate / jnp.expand_dims(scale_gate, 1)).astype(jnp.bfloat16),
        (train_up / jnp.expand_dims(scale_up, 1)).astype(jnp.bfloat16),
        (train_down / jnp.expand_dims(scale_down, 2)).astype(jnp.bfloat16),
    )
    ready_gate, ready_up = (
        lax.all_to_all(narrow_gate, "rows", split_axis=2, concat_axis=1, tiled=True),
        lax.all_to_all(narrow_up, "rows", split_axis=2, concat_axis=1, tiled=True),
    )
    ready_down = lax.all_to_all(narrow_down, "rows", split_axis=1, concat_axis=2, tiled=True)
    scale_gate = lax.dynamic_slice_in_dim(
        scale_gate, lax.axis_index("rows") * ready_gate.shape[2], ready_gate.shape[2], axis=1
    )
    scale_up = lax.dynamic_slice_in_dim(
        scale_up, lax.axis_index("rows") * ready_up.shape[2], ready_up.shape[2], axis=1
    )
    scale_down = lax.dynamic_slice_in_dim(
        scale_down, lax.axis_index("rows") * ready_down.shape[1], ready_down.shape[1], axis=1
    )
    part_router = (router_weight * router_gain[:, None]).astype(jnp.bfloat16)
    row_router = lax.all_gather(part_router, "rows", axis=0, tiled=True)
    serve_router = lax.all_gather(row_router, "owner", axis=1, tiled=True)
    return (ready_gate, ready_up, ready_down, scale_gate, scale_up, scale_down, serve_router)


def solution(mesh):
    return jax.shard_map(
        local,
        mesh=mesh,
        in_specs=(
            P("owner", "rows", None),
            P("owner", "rows", None),
            P("owner", None, "rows"),
            P("rows", "owner"),
            P("rows"),
        ),
        out_specs=(
            P("owner", None, "rows"),
            P("owner", None, "rows"),
            P("owner", "rows", None),
            P("owner", "rows"),
            P("owner", "rows"),
            P("owner", "rows"),
            P(),
        ),
        check_vma=False,
    )
```

profile of v0, /device:TPU:0, one launch (start us, length us, event | category | flops | bytes accessed | tf_op | source)
XLA Modules:
  0.0 737.8 jit_solution(7608499507201470121)
XLA Ops:
  7.2 0.0 all-reduce.3.cloned.1.call-start
  7.2 8.6 %abs_reduce_fusion = f32[16,1024]{1,0:T(8,128)} fusion(f32[16,1024,256]{2,1,0:T(8,128)} %param.7), kind=kLoop, calls=%fused_computation.2 | loop fusion | flops 8372224 | bytes 16842752 | tf_op jit(solution)/shard_map/reduce_sum | solution.py:14
  15.8 12.6 %abs_reduce_fusion.1 = (f32[16,1024]{1,0:T(8,128)}, f32[16,1024]{1,0:T(8,128)}) fusion(f32[16,256,1024]{2,1,0:T(8,128)} %param.6, f32[16,256,1024]{2,1,0:T(8,128)} %param.5), kind=kLoop, calls=%fused_computation.4 | loop fusion | flops 16744448 | bytes 33685504 | tf_op jit(solution)/shard_map/reduce_sum | solution.py:13
  28.4 0.0 all-reduce.3.cloned.1.call-update
  28.4 17.6 %copy.19 = f32[16,256,1024]{1,0,2:T(8,128)} copy(f32[16,256,1024]{2,1,0:T(8,128)} %param.6) | data formatting | bytes 33554432 | tf_op args[1]
  46.1 40.7 %all-reduce.3.cloned.1.call-done = (f32[16,1024]{1,0:T(8,128)}, f32[16,1024]{1,0:T(8,128)}, f32[16,1024]{1,0:T(8,128)}) async-done(((f32[16,1024]{1,0:T(8,128)}, f32[16,1024]{1,0:T(8,128)}, f32[16,1024]{1,0:T(8,128)}), (f32[16,1024]{1,0:T(8,128)}, f32[16,1024]{1,0:T(8,128)}, f32[16,1024]{1,0:T(8,128)})) %all-reduce.3.cloned.1.call-update) | async-done | bytes 196624 | tf_op jit(solution)/shard_map/psum | solution.py:10
  86.8 0.8 broadcast_multiply_fusion.1
  87.6 0.2 copy.18
  87.8 9.6 %divide_convert_fusion = bf16[16,256,1024]{1,0,2:T(8,128)(2,1)} fusion(f32[16,256,1024]{1,0,2:T(8,128)} %copy.19, f32[16,1024]{0,1:T(8,128)S(1)} %copy.18), kind=kLoop, calls=%fused_computation.3 | loop fusion | flops 8388608 | bytes 25231360 | tf_op jit(solution)/shard_map/convert_element_type | solution.py:23
  97.5 4.9 all-to-all-start.1
  102.4 0.0 copy-start.1
  102.4 17.6 %copy.16 = f32[16,256,1024]{1,0,2:T(8,128)} copy(f32[16,256,1024]{2,1,0:T(8,128)} %param.5) | data formatting | bytes 33554432 | tf_op args[0]
  120.0 0.0 copy-done.1
  120.0 0.2 copy.15
  120.2 0.0 copy-start
  120.3 9.7 %divide_convert_fusion.1 = bf16[16,256,1024]{1,0,2:T(8,128)(2,1)} fusion(f32[16,256,1024]{1,0,2:T(8,128)} %copy.16, f32[16,1024]{0,1:T(8,128)S(1)} %copy.15), kind=kLoop, calls=%fused_computation.5 | loop fusion | flops 8388608 | bytes 25231360 | tf_op jit(solution)/shard_map/convert_element_type | solution.py:22
  129.9 156.3 %all-to-all-done.1 = bf16[16,256,1024]{1,0,2:T(8,128)(2,1)} async-done(((bf16[16,256,1024]{1,0,2:T(8,128)(2,1)}), bf16[16,256,1024]{1,0,2:T(8,128)(2,1)}, u32[]{:S(2)}, u32[]{:S(2)}) %all-to-all-start.1) | async-done | bytes 8388640 | tf_op jit(solution)/shard_map/all_to_all | solution.py:28
  286.3 4.9 all-to-all-start
  291.2 0.0 copy-done
  291.2 0.2 copy.21
  291.4 0.0 copy-start.2
  291.4 0.0 copy-start.3
  291.5 16.6 %fusion = bf16[16,1024,256]{2,0,1:T(8,128)(2,1)} fusion(f32[16,1024,256]{2,1,0:T(8,128)} %param.7, f32[16,1024]{0,1:T(8,128)S(1)} %copy.21), kind=kLoop, calls=%fused_computation.1 | loop fusion | flops 8388608 | bytes 25231360 | tf_op jit(solution)/shard_map/convert_element_type | solution.py:24
  308.1 167.0 %all-to-all-done = bf16[16,256,1024]{1,0,2:T(8,128)(2,1)} async-done(((bf16[16,256,1024]{1,0,2:T(8,128)(2,1)}), bf16[16,256,1024]{1,0,2:T(8,128)(2,1)}, u32[]{:S(2)}, u32[]{:S(2)}) %all-to-all-start) | async-done | bytes 8388640 | tf_op jit(solution)/shard_map/all_to_all | solution.py:27
  475.1 5.0 all-to-all-start.2
  480.1 0.0 copy-done.2
  480.1 0.0 copy-done.3
  480.1 189.9 %all_gather.6 = bf16[2048,16]{0,1:T(8,128)(2,1)S(1)} all-gather(bf16[256,16]{0,1:T(8,128)(2,1)S(1)} %multiply_convert_fusion), channel_id=1, replica_groups=mesh['owner'=4,'rows'=8] {'rows'}, dimensions={0}, use_global_device_ids=true | all-gather | bytes 73728 | tf_op jit(solution)/shard_map/all_gather | solution.py:41
  670.0 9.1 %all_gather.7 = bf16[2048,64]{0,1:T(8,128)(2,1)S(1)} all-gather(bf16[2048,16]{0,1:T(8,128)(2,1)S(1)} %all_gather.6), channel_id=1, replica_groups=mesh['owner'=4,'rows'=8] {'owner'}, dimensions={1}, use_global_device_ids=true | all-gather | bytes 327680 | tf_op jit(solution)/shard_map/all_gather | solution.py:42
  679.1 0.6 constant_dynamic-slice_fusion
  679.7 0.6 constant_dynamic-slice_fusion.1
  680.3 0.6 constant_dynamic-slice_fusion.2
  680.9 12.3 %copy.20 = bf16[16,8,256,128]{3,2,1,0:T(8,128)(2,1)} copy(bf16[16,8,256,128]{2,0,3,1:T(8,128)(2,1)} %bitcast.4) | data formatting | bytes 16777216 | tf_op jit(solution)/shard_map/all_to_all | solution.py:28
  693.2 12.3 %copy.17 = bf16[16,8,256,128]{3,2,1,0:T(8,128)(2,1)} copy(bf16[16,8,256,128]{2,0,3,1:T(8,128)(2,1)} %bitcast.1) | data formatting | bytes 16777216 | tf_op jit(solution)/shard_map/all_to_all | solution.py:27
  705.5 0.0 all-to-all-done.2
  705.5 11.4 %copy.23 = bf16[16,128,8,256]{3,2,1,0:T(8,128)(2,1)} copy(bf16[16,128,8,256]{3,0,1,2:T(8,128)(2,1)} %bitcast.7) | data formatting | bytes 16777216 | tf_op jit(solution)/shard_map/all_to_all | solution.py:30
  716.9 13.4 %all_to_all.50 = bf16[16,128,2048]{2,1,0:T(8,128)(2,1)} reshape(bf16[16,128,8,256]{3,2,1,0:T(8,128)(2,1)} %copy.23) | data formatting | bytes 16777216 | tf_op jit(solution)/shard_map/all_to_all | solution.py:30
  730.3 0.7 copy.31
  (3 shorter events, 0.0 us)
Async XLA Ops:
  7.2 79.6 %all-reduce.3.cloned.1.call-start = ((), (), s32[]{:S(2)}) async-start(), calls=%async_computation.3 | async-start | bytes 393216 | tf_op jit(solution)/shard_map/psum | solution.py:10
  97.5 188.8 %all-to-all-start.1 = ((bf16[16,256,1024]{1,0,2:T(8,128)(2,1)}), bf16[16,256,1024]{1,0,2:T(8,128)(2,1)}, u32[]{:S(2)}, u32[]{:S(2)}) async-start(bf16[16,256,1024]{1,0,2:T(8,128)(2,1)} %divide_convert_fusion), calls=%async_computation.1 | async-start | bytes 16777216 | tf_op jit(solution)/shard_map/all_to_all | solution.py:28
  102.4 17.6 %copy-start.1 = (f32[16,1024]{1,0:T(8,128)S(1)}, f32[16,1024]{1,0:T(8,128)}, u32[]{:S(2)}) copy-start(f32[16,1024]{1,0:T(8,128)} %get-tuple-element.7) | copy-start | bytes 196612
  120.2 171.0 %copy-start = (f32[16,1024]{1,0:T(8,128)S(1)}, f32[16,1024]{1,0:T(8,128)}, u32[]{:S(2)}) copy-start(f32[16,1024]{1,0:T(8,128)} %get-tuple-element.9) | copy-start | bytes 196612
  286.3 188.8 %all-to-all-start = ((bf16[16,256,1024]{1,0,2:T(8,128)(2,1)}), bf16[16,256,1024]{1,0,2:T(8,128)(2,1)}, u32[]{:S(2)}, u32[]{:S(2)}) async-start(bf16[16,256,1024]{1,0,2:T(8,128)(2,1)} %divide_convert_fusion.1), calls=%async_computation | async-start | bytes 16777216 | tf_op jit(solution)/shard_map/all_to_all | solution.py:27
  291.4 188.7 %copy-start.2 = (f32[256,16]{0,1:T(8,128)S(1)}, f32[256,16]{0,1:T(8,128)}, u32[]{:S(2)}) copy-start(f32[256,16]{0,1:T(8,128)} %param.8) | copy-start | bytes 49156
  291.4 188.7 %copy-start.3 = (f32[256]{0:T(256)S(1)}, f32[256]{0:T(256)}, u32[]{:S(2)}) copy-start(f32[256]{0:T(256)} %param.9) | copy-start | bytes 3076
  475.1 230.4 %all-to-all-start.2 = ((bf16[16,1024,256]{2,0,1:T(8,128)(2,1)}), bf16[16,1024,256]{2,0,1:T(8,128)(2,1)}, u32[]{:S(2)}, u32[]{:S(2)}) async-start(bf16[16,1024,256]{2,0,1:T(8,128)(2,1)} %fusion), calls=%async_computation.2 | async-start | bytes 16777216 | tf_op jit(solution)/shard_map/all_to_all | solution.py:30
Sparse Core Ops, SparseCore 0:
  28.6 58.1 all-reduce.2
where the time goes:
time: 740 us; the launch traced here: 738 us
  waiting for transfers between devices  364 us (49%)
  blocking collectives  199 us (27%)
  local copies, waits for them, and re-layouts  87.7 us (12%)
  other arithmetic  58 us (8%)
  starting transfers between devices  14.9 us (2%)
  between operations  14.2 us (2%)
    all_gather x1, blocking collectives, local(): row_router = lax.all_gather(part_router, 'rows', axis=0, tiled=True)  190 us
    all_to_all x1, waiting for transfers between devices, local(): lax.all_to_all(narrow_gate, 'rows', split_axis=2, concat_axis=1, tiled=True)  167 us
    all_to_all x1, waiting for transfers between devices, local(): lax.all_to_all(narrow_up, 'rows', split_axis=2, concat_axis=1, tiled=True)  156 us
    psum x1, waiting for transfers between devices, local(): lax.psum((jnp.sum(jnp.abs(train_gate), axis=1), jnp.sum(jnp.abs(train_up)...  40.7 us
    unnamed x11, local copies, waits for them, and re-layouts  36 us
    all_to_all x2, local copies, waits for them, and re-layouts, local(): lax.all_to_all(narrow_down, 'rows', split_axis=1, concat_axis=2, tiled=True)  24.8 us
    convert_element_type x1, other arithmetic, local(): (train_down / jnp.expand_dims(scale_down, 2)).astype(jnp.bfloat16)  16.6 us
  transfers between devices with their start and end apart: 4, of which 3 were waited for; matrix products, arithmetic and copies ran while one was open for 12% of the time, Pallas kernels for 0%

commit v1 on v0

--- a/solution.py
+++ b/solution.py
@@ -4,6 +4,19 @@
 from jax.sharding import PartitionSpec as P
 
 D_MODEL = 2048
+
+
+def see_gates_in(x_in, in_dim, dim_no):
+    main = jnp.concatenate(
+        jax.lax.all_to_all(
+            jnp.stack(jnp.split(x_in, jax.lax.axis_size("rows"), in_dim), 0),
+            "rows",
+            split_axis=0,
+            concat_axis=0,
+        ),
+        dim_no,
+    )
+    return main
 
 
 def local(train_gate, train_up, train_down, router_weight, router_gain):
@@ -24,7 +37,7 @@
         (train_down / jnp.expand_dims(scale_down, 2)).astype(jnp.bfloat16),
     )
     ready_gate, ready_up = (
-        lax.all_to_all(narrow_gate, "rows", split_axis=2, concat_axis=1, tiled=True),
+        see_gates_in(narrow_gate, 2, 1),
         lax.all_to_all(narrow_up, "rows", split_axis=2, concat_axis=1, tiled=True),
     )
     ready_down = lax.all_to_all(narrow_down, "rows", split_axis=1, concat_axis=2, tiled=True)

time: 740 us -> 742 us (level)
  waiting for transfers between devices: 364 us -> 382 us
  local copies, waits for them, and re-layouts: 87.7 us -> 75.5 us
    psum x1, waiting for transfers between devices: 40.7 us -> 58.3 us  [local(): lax.psum((jnp.sum(jnp.abs(train_gate), axis=1), jnp.sum(jnp.abs(train_up)...]
    all_to_all x1 -> x0, local copies, waits for them, and re-layouts: 12.3 us -> none  [local(): lax.all_to_all(narrow_gate, 'rows', split_axis=2, concat_axis=1, tiled=True)]
    all_to_all x1, waiting for transfers between devices: 156 us -> 167 us  [local(): lax.all_to_all(narrow_up, 'rows', split_axis=2, concat_axis=1, tiled=True)]
    all_to_all x1, waiting for transfers between devices: 167 us -> 156 us  [see_gates_in(): jax.lax.all_to_all(jnp.stack(jnp.split(x_in, jax.lax.axis_size('rows'), i...]
    unnamed x11 -> x17, local copies, waits for them, and re-layouts: 36 us -> 27.1 us
    reshape x0 -> x1, local copies, waits for them, and re-layouts: none -> 7.89 us  [see_gates_in(): jnp.concatenate(jax.lax.all_to_all(jnp.stack(jnp.split(x_in, jax.lax.axis...]
  transfers between devices with their start and end apart: 4 -> 4, of which waited for: 3 -> 3; matrix products, arithmetic and copies ran while one was open for 12% -> 9% of each run, Pallas kernels for 0% -> 0%
where the time goes in v1:
time: 742 us; the launch traced here: 741 us
  waiting for transfers between devices  382 us (51%)
  blocking collectives  199 us (27%)
  local copies, waits for them, and re-layouts  75.5 us (10%)
  other arithmetic  55.6 us (7%)
  starting transfers between devices  15.1 us (2%)
  between operations  14.1 us (2%)
    all_gather x1, blocking collectives, local(): row_router = lax.all_gather(part_router, 'rows', axis=0, tiled=True)  190 us
    all_to_all x1, waiting for transfers between devices, local(): lax.all_to_all(narrow_up, 'rows', split_axis=2, concat_axis=1, tiled=True)  167 us
    all_to_all x1, waiting for transfers between devices, see_gates_in(): jax.lax.all_to_all(jnp.stack(jnp.split(x_in, jax.lax.axis_size('rows'), i...  156 us
    psum x1, waiting for transfers between devices, local(): lax.psum((jnp.sum(jnp.abs(train_gate), axis=1), jnp.sum(jnp.abs(train_up)...  58.3 us
    unnamed x17, local copies, waits for them, and re-layouts  27.1 us
    all_to_all x2, local copies, waits for them, and re-layouts, local(): lax.all_to_all(narrow_down, 'rows', split_axis=1, concat_axis=2, tiled=True)  24.8 us
    convert_element_type x1, other arithmetic, local(): (train_down / jnp.expand_dims(scale_down, 2)).astype(jnp.bfloat16)  16.6 us
  transfers between devices with their start and end apart: 4, of which 3 were waited for; matrix products, arithmetic and copies ran while one was open for 9% of the time, Pallas kernels for 0%

profile of v1, /device:TPU:0, one launch (start us, length us, event | category | flops | bytes accessed | tf_op | source)
XLA Modules:
  0.0 740.8 jit_solution(12766531883530185823)
XLA Ops:
  7.2 0.0 all-reduce.3.cloned.1.call-start
  7.2 8.6 %abs_reduce_fusion = f32[16,1024]{1,0:T(8,128)} fusion(f32[16,1024,256]{2,1,0:T(8,128)} %param.7), kind=kLoop, calls=%fused_computation.2 | loop fusion | flops 8372224 | bytes 16842752 | tf_op jit(solution)/shard_map/reduce_sum | solution.py:27
  15.8 12.6 %abs_reduce_fusion.1 = (f32[16,1024]{1,0:T(8,128)}, f32[16,1024]{1,0:T(8,128)}) fusion(f32[16,256,1024]{2,1,0:T(8,128)} %param.6, f32[16,256,1024]{2,1,0:T(8,128)} %param.5), kind=kLoop, calls=%fused_computation.4 | loop fusion | flops 16744448 | bytes 33685504 | tf_op jit(solution)/shard_map/reduce_sum | solution.py:26
  28.4 0.0 all-reduce.3.cloned.1.call-update
  28.4 58.3 %all-reduce.3.cloned.1.call-done = (f32[16,1024]{1,0:T(8,128)}, f32[16,1024]{1,0:T(8,128)}, f32[16,1024]{1,0:T(8,128)}) async-done(((f32[16,1024]{1,0:T(8,128)}, f32[16,1024]{1,0:T(8,128)}, f32[16,1024]{1,0:T(8,128)}), (f32[16,1024]{1,0:T(8,128)}, f32[16,1024]{1,0:T(8,128)}, f32[16,1024]{1,0:T(8,128)})) %all-reduce.3.cloned.1.call-update) | async-done | bytes 196624 | tf_op jit(solution)/shard_map/psum | solution.py:23
  86.8 0.8 broadcast_multiply_fusion.2
  87.6 7.2 divide_convert_fusion.1
  94.8 1.2 fusion.8
  96.1 1.2 fusion.7
  97.3 1.2 fusion.6
  98.6 1.2 fusion.5
  99.8 1.2 fusion.4
  101.1 1.2 fusion.3
  102.3 1.2 fusion.2
  103.6 1.2 fusion.1
  104.8 4.9 all-to-all-start
  109.8 0.0 copy-start.1
  109.8 17.6 %copy.17 = f32[16,256,1024]{1,0,2:T(8,128)} copy(f32[16,256,1024]{2,1,0:T(8,128)} %param.6) | data formatting | bytes 33554432 | tf_op args[1]
  127.4 0.0 copy-done.1
  127.4 0.2 copy.16
  127.6 9.6 %divide_convert_fusion = bf16[16,256,1024]{1,0,2:T(8,128)(2,1)} fusion(f32[16,256,1024]{1,0,2:T(8,128)} %copy.17, f32[16,1024]{0,1:T(8,128)S(1)} %copy.16), kind=kLoop, calls=%fused_computation.3 | loop fusion | flops 8388608 | bytes 25231360 | tf_op jit(solution)/shard_map/convert_element_type | solution.py:36
  137.3 0.0 copy-start
  137.3 156.4 %all-to-all-done = bf16[8,16,256,128]{3,2,1,0:T(8,128)(2,1)} async-done(((bf16[8,16,256,128]{3,2,1,0:T(8,128)(2,1)}), bf16[8,16,256,128]{3,2,1,0:T(8,128)(2,1)}, u32[]{:S(2)}, u32[]{:S(2)}) %all-to-all-start) | async-done | bytes 8388640 | tf_op jit(solution)/shard_map/all_to_all | solution.py:11
  293.6 4.9 all-to-all-start.1
  298.6 0.0 copy-done
  298.6 0.2 copy.19
  298.8 16.6 %fusion = bf16[16,1024,256]{2,0,1:T(8,128)(2,1)} fusion(f32[16,1024,256]{2,1,0:T(8,128)} %param.7, f32[16,1024]{0,1:T(8,128)S(1)} %copy.19), kind=kLoop, calls=%fused_computation.1 | loop fusion | flops 8388608 | bytes 25231360 | tf_op jit(solution)/shard_map/convert_element_type | solution.py:37
  315.5 0.0 copy-start.2
  315.5 0.0 copy-start.3
  315.5 167.0 %all-to-all-done.1 = bf16[16,256,1024]{1,0,2:T(8,128)(2,1)} async-done(((bf16[16,256,1024]{1,0,2:T(8,128)(2,1)}), bf16[16,256,1024]{1,0,2:T(8,128)(2,1)}, u32[]{:S(2)}, u32[]{:S(2)}) %all-to-all-start.1) | async-done | bytes 8388640 | tf_op jit(solution)/shard_map/all_to_all | solution.py:41
  482.4 5.2 all-to-all-start.2
  487.7 0.0 copy-done.2
  487.7 0.0 copy-done.3
  487.7 189.9 %all_gather.6 = bf16[2048,16]{0,1:T(8,128)(2,1)S(1)} all-gather(bf16[256,16]{0,1:T(8,128)(2,1)S(1)} %multiply_convert_fusion), channel_id=1, replica_groups=mesh['owner'=4,'rows'=8] {'rows'}, dimensions={0}, use_global_device_ids=true | all-gather | bytes 73728 | tf_op jit(solution)/shard_map/all_gather | solution.py:54
  677.6 8.9 %all_gather.7 = bf16[2048,64]{0,1:T(8,128)(2,1)S(1)} all-gather(bf16[2048,16]{0,1:T(8,128)(2,1)S(1)} %all_gather.6), channel_id=1, replica_groups=mesh['owner'=4,'rows'=8] {'owner'}, dimensions={1}, use_global_device_ids=true | all-gather | bytes 327680 | tf_op jit(solution)/shard_map/all_gather | solution.py:55
  686.5 0.6 constant_dynamic-slice_fusion
  687.1 0.6 constant_dynamic-slice_fusion.1
  687.7 0.6 constant_dynamic-slice_fusion.2
  688.3 7.9 %copy.15 = bf16[16,8,256,128]{3,2,1,0:T(8,128)(2,1)} copy(bf16[16,8,256,128]{3,2,0,1:T(8,128)(2,1)} %bitcast.8) | data formatting | bytes 16777216 | tf_op jit(solution)/shard_map/reshape | solution.py:10
  696.2 12.3 %copy.18 = bf16[16,8,256,128]{3,2,1,0:T(8,128)(2,1)} copy(bf16[16,8,256,128]{2,0,3,1:T(8,128)(2,1)} %bitcast.11) | data formatting | bytes 16777216 | tf_op jit(solution)/shard_map/all_to_all | solution.py:41
  708.5 0.0 all-to-all-done.2
  708.5 11.4 %copy.21 = bf16[16,128,8,256]{3,2,1,0:T(8,128)(2,1)} copy(bf16[16,128,8,256]{3,0,1,2:T(8,128)(2,1)} %bitcast.14) | data formatting | bytes 16777216 | tf_op jit(solution)/shard_map/all_to_all | solution.py:43
  719.8 13.4 %all_to_all.37 = bf16[16,128,2048]{2,1,0:T(8,128)(2,1)} reshape(bf16[16,128,8,256]{3,2,1,0:T(8,128)(2,1)} %copy.21) | data formatting | bytes 16777216 | tf_op jit(solution)/shard_map/all_to_all | solution.py:43
  733.3 0.7 copy.36
  (3 shorter events, 0.0 us)
Async XLA Ops:
  7.2 79.6 %all-reduce.3.cloned.1.call-start = ((), (), s32[]{:S(2)}) async-start(), calls=%async_computation.3 | async-start | bytes 393216 | tf_op jit(solution)/shard_map/psum | solution.py:23
  104.8 188.8 %all-to-all-start = ((bf16[8,16,256,128]{3,2,1,0:T(8,128)(2,1)}), bf16[8,16,256,128]{3,2,1,0:T(8,128)(2,1)}, u32[]{:S(2)}, u32[]{:S(2)}) async-start(bf16[8,16,256,128]{3,2,1,0:T(8,128)(2,1)} %fusion.1), calls=%async_computation | async-start | bytes 16777216 | tf_op jit(solution)/shard_map/all_to_all | solution.py:11
  109.8 17.6 %copy-start.1 = (f32[16,1024]{1,0:T(8,128)S(1)}, f32[16,1024]{1,0:T(8,128)}, u32[]{:S(2)}) copy-start(f32[16,1024]{1,0:T(8,128)} %get-tuple-element.8) | copy-start | bytes 196612
  137.3 161.3 %copy-start = (f32[16,1024]{1,0:T(8,128)S(1)}, f32[16,1024]{1,0:T(8,128)}, u32[]{:S(2)}) copy-start(f32[16,1024]{1,0:T(8,128)} %get-tuple-element.9) | copy-start | bytes 196612
  293.6 188.8 %all-to-all-start.1 = ((bf16[16,256,1024]{1,0,2:T(8,128)(2,1)}), bf16[16,256,1024]{1,0,2:T(8,128)(2,1)}, u32[]{:S(2)}, u32[]{:S(2)}) async-start(bf16[16,256,1024]{1,0,2:T(8,128)(2,1)} %divide_convert_fusion), calls=%async_computation.1 | async-start | bytes 16777216 | tf_op jit(solution)/shard_map/all_to_all | solution.py:41
  315.5 172.2 %copy-start.2 = (f32[256,16]{0,1:T(8,128)S(1)}, f32[256,16]{0,1:T(8,128)}, u32[]{:S(2)}) copy-start(f32[256,16]{0,1:T(8,128)} %param.8) | copy-start | bytes 49156
  315.5 172.2 %copy-start.3 = (f32[256]{0:T(256)S(1)}, f32[256]{0:T(256)}, u32[]{:S(2)}) copy-start(f32[256]{0:T(256)} %param.9) | copy-start | bytes 3076
  482.4 226.0 %all-to-all-start.2 = ((bf16[16,1024,256]{2,0,1:T(8,128)(2,1)}), bf16[16,1024,256]{2,0,1:T(8,128)(2,1)}, u32[]{:S(2)}, u32[]{:S(2)}) async-start(bf16[16,1024,256]{2,0,1:T(8,128)(2,1)} %fusion), calls=%async_computation.2 | async-start | bytes 16777216 | tf_op jit(solution)/shard_map/all_to_all | solution.py:43
Sparse Core Ops, SparseCore 0:
  28.6 58.1 all-reduce.2
